TPU v7x, 32 devices: a whole 2x2x4 slice. The times are simulated.
32 devices in a mesh: space: 16 (over z, y, x), rep: 2 (over core).
Axes of the slice: x: 2, y: 2, z: 4, core: 2. Of those that a mesh axis runs over, the one named last changes fastest.
Arguments:
- halo_rows: bfloat16 [4, 2048, 256], P(None, 'space', 'rep'), may hold values from -6 to 6
- unmatched: int32 [4, 2048], P(None, 'space'), may hold values 0 or 1
- owner_id: int32 [4, 2048, 1], P(None, 'space'), may hold values from 0 to 15; in each aligned block of 128 rows (0 to 127, 128 to 255, ..., all dimensions but the last counted through in order) at most 16 rows name the same one
- cand_index: int32 [4, 2048, 16], P(None, 'space'), may hold values from 0 to 511
- lengths: int32 [4, 2048], P(None, 'space'), may hold values from 1 to 16
- choice_index: int32 [4, 2048], P(None, 'space'), may hold values from 0 to 15, as said below
- desc_rows: bfloat16 [4, 8192, 256], P(None, 'space', 'rep'), may hold values from -6 to 6
Outputs:
- phantom: bfloat16 [4, 2048, 256], P(None, 'space', 'rep')
- best_merit: bfloat16 [4, 2048], P(None, 'space')
Inputs may be any that keep to these rules, and one draw needn't show every extreme that they name: `owner_id`: in each aligned block of 128 halos (one region in one snapshot) no owner is named by more than 16 halos, a bound that some block reaches. `choice_index`: less than the halo's length.
All inputs are finite; a program needn't handle non-finite values. No bound on the sum of `unmatched` on one device may be relied on, other than what follows from the above.
Results may differ from a plain program's by a relative error of at most 0.001.
Values may be sent and summed in bfloat16 or wider, within the bound.
A program may use at most 64 MiB of HBM per device.

v0:
```python
import math

import jax
import jax.numpy as jnp
from jax import lax
from jax.sharding import PartitionSpec as P

WIDTH = 256
K = 16


def route_snapshot(rows_here, live_here, dest_owner, listing, span, picks, peer_count, slot_count):
    slot_total = peer_count * slot_count
    halo_count, half_width = rows_here.shape
    peer_ids = jnp.arange(peer_count, dtype=jnp.int32)
    onehot = (dest_owner[:, None] == peer_ids[None, :]).astype(jnp.bfloat16)
    halo_ids = jnp.arange(halo_count, dtype=jnp.int32)
    lower = (halo_ids[:, None] >= halo_ids[None, :]).astype(jnp.bfloat16)
    prefix = jnp.dot(lower, onehot, preferred_element_type=jnp.float32)
    slot_rank = (jnp.sum(prefix * onehot.astype(jnp.float32), axis=1) - 1.0).astype(jnp.int32)
    target = dest_owner * slot_count + slot_rank
    meta_rows = jnp.concatenate(
        [listing, live_here[:, None], span[:, None], picks[:, None]], axis=1
    )
    send_rows = jnp.zeros((slot_total, half_width), jnp.bfloat16).at[target].set(rows_here)
    send_meta = jnp.zeros((slot_total, K + 3), jnp.int32).at[target].set(meta_rows)
    return (
        send_rows.reshape(peer_count, slot_count, half_width),
        send_meta.reshape(peer_count, slot_count, K + 3),
        target,
    )


def score_requests(got_rows, got_meta, desc_table):
    slot_total, half_width = got_rows.shape
    block_size = min(512, slot_total)
    listed = got_meta[:, :K]

    def score_block(pieces):
        rows_block, index_block = pieces
        tile_scores = jnp.einsum(
            "rw,cw->rc", rows_block, desc_table, preferred_element_type=jnp.float32
        )
        return jnp.take_along_axis(tile_scores, index_block, axis=1)

    partial_merit = lax.map(
        score_block,
        (got_rows.reshape(-1, block_size, half_width), listed.reshape(-1, block_size, K)),
    ).reshape(slot_total, K)
    return partial_merit


def settle_requests(summed, got_rows, got_meta, desc_table, peer_count, slot_count):
    lane_ids = jnp.arange(K, dtype=jnp.int32)
    listed = got_meta[:, :K]
    live_flag = got_meta[:, K]
    length_got = got_meta[:, K + 1]
    pick_pos = got_meta[:, K + 2 : K + 3]
    merit_full = summed / math.sqrt(WIDTH)
    used = lane_ids[None, :] < length_got[:, None]
    live_entry = used & (live_flag[:, None] == 1)
    quality = 1.0 + jax.nn.softplus(merit_full)
    claims = (
        jnp.zeros((desc_table.shape[0],), jnp.float32)
        .at[listed.reshape(-1)]
        .max(jnp.where(live_entry, quality, jnp.zeros_like(quality)).reshape(-1))
    )
    chosen = jnp.take_along_axis(listed, pick_pos, 1)[:, 0]
    chosen_quality = jnp.take_along_axis(quality, pick_pos, 1)[:, 0]
    share_weight = chosen_quality / (chosen_quality + claims[chosen])
    blended = (
        (1.0 - share_weight)[:, None] * got_rows.astype(jnp.float32)
        + share_weight[:, None] * desc_table[chosen].astype(jnp.float32)
    ).astype(jnp.bfloat16)
    top_merit = jnp.max(jnp.where(used, merit_full, jnp.full_like(merit_full, -1e30)), axis=1)
    top_merit = jnp.where(live_flag == 1, top_merit, jnp.zeros_like(top_merit)).astype(jnp.bfloat16)
    return (blended.reshape(peer_count, slot_count, -1), top_merit.reshape(peer_count, slot_count))


def land_replies(back_rows, back_best, target, rows_here, live_here):
    slot_total = back_best.size
    back_rows = back_rows.reshape(slot_total, -1)[target]
    back_best = back_best.reshape(slot_total)[target]
    live_halo = live_here == 1
    return (
        jnp.where(live_halo[:, None], back_rows, rows_here),
        jnp.where(live_halo, back_best, jnp.zeros_like(back_best)),
    )


def body(halo_rows, unmatched, owner_id, cand_index, lengths, choice_index, desc_rows):
    peer_count = lax.axis_size("space")
    snap_count, halo_count, half_width = halo_rows.shape
    slot_count = 2 * halo_count // peer_count
    slot_total = peer_count * slot_count
    phantom_list = []
    best_list = []
    routed = [
        route_snapshot(
            halo_rows[snapshot],
            unmatched[snapshot],
            owner_id[snapshot, :, 0],
            cand_index[snapshot],
            lengths[snapshot],
            choice_index[snapshot],
            peer_count,
            slot_count,
        )
        for snapshot in range(snap_count)
    ]
    all_rows = jnp.stack([item[0] for item in routed])
    all_meta = jnp.stack([item[1] for item in routed])
    got_rows_all, got_meta_all = (
        lax.all_to_all(all_rows, "space", split_axis=1, concat_axis=1, tiled=True),
        lax.all_to_all(all_meta, "space", split_axis=1, concat_axis=1, tiled=True),
    )
    got_rows_all = got_rows_all.reshape(snap_count, slot_total, half_width)
    got_meta_all = got_meta_all.reshape(snap_count, slot_total, K + 3)
    partial_all = jnp.stack(
        [
            score_requests(got_rows_all[snapshot], got_meta_all[snapshot], desc_rows[snapshot])
            for snapshot in range(snap_count)
        ]
    )
    summed_all = lax.psum(partial_all, "rep")
    settled = [
        settle_requests(
            summed_all[snapshot],
            got_rows_all[snapshot],
            got_meta_all[snapshot],
            desc_rows[snapshot],
            peer_count,
            slot_count,
        )
        for snapshot in range(snap_count)
    ]
    blended_all = jnp.stack([item[0] for item in settled])
    top_all = jnp.stack([item[1] for item in settled])
    back_rows_all, back_best_all = (
        lax.all_to_all(blended_all, "space", split_axis=1, concat_axis=1, tiled=True),
        lax.all_to_all(top_all, "space", split_axis=1, concat_axis=1, tiled=True),
    )
    for snapshot in range(snap_count):
        phantom_one, best_one = land_replies(
            back_rows_all[snapshot],
            back_best_all[snapshot],
            routed[snapshot][2],
            halo_rows[snapshot],
            unmatched[snapshot],
        )
        phantom_list.append(phantom_one)
        best_list.append(best_one)
    return (jnp.stack(phantom_list), jnp.stack(best_list))


def solution(mesh):
    in_specs = (
        P(None, "space", "rep"),
        P(None, "space"),
        P(None, "space", None),
        P(None, "space", None),
        P(None, "space"),
        P(None, "space"),
        P(None, "space", "rep"),
    )
    out_specs = (P(None, "space", "rep"), P(None, "space"))
    return jax.shard_map(body, mesh=mesh, in_specs=in_specs, out_specs=out_specs, check_vma=False)
```

profile of v0, /device:TPU:0, one launch (start us, length us, event | category | flops | bytes accessed | tf_op | source)
XLA Modules:
  0.0 399.2 jit_solution(855775819349534204)
XLA Ops:
  10.2 0.9 slice_bitcast_fusion.23
  12.8 0.9 scatter_custom_fusion.4
  13.9 0.9 scatter_custom_fusion.6
  15.1 0.9 scatter_custom_fusion.7
  16.3 0.9 scatter_custom_fusion.5
  18.0 1.1 reshape.1189
  19.1 8.5 %all-to-all-start.1 = ((s32[16,1,1216]{2,1,0:T(1,128)}), s32[16,1,1216]{2,1,0:T(1,128)S(1)}, u32[]{:S(2)}, u32[]{:S(2)}) async-start(s32[16,1,1216]{2,1,0:T(1,128)} %reshape.1189), calls=%async_computation.1 | async-start | bytes 163840 | tf_op jit(solution)/shard_map/all_to_all | solution.py:115
  29.5 0.9 scatter_custom_fusion
  30.4 0.9 scatter_custom_fusion.2
  31.3 0.9 scatter_custom_fusion.3
  32.2 0.9 scatter_custom_fusion.1
  33.9 1.3 all-to-all-done.1
  35.2 5.6 %all-to-all-start = ((bf16[4,16,16,128]{3,2,0,1:T(8,128)(2,1)}), bf16[4,16,16,128]{3,2,0,1:T(8,128)(2,1)S(1)}, u32[]{:S(2)}, u32[]{:S(2)}) async-start(bf16[4,16,16,128]{3,2,0,1:T(8,128)(2,1)} %pad_maximum_fusion), calls=%async_computation | async-start | bytes 524288 | tf_op jit(solution)/shard_map/all_to_all | solution.py:114
  41.5 0.8 reduce.56
  53.5 2.4 gather_fusion.21
  56.0 2.4 gather_fusion.23
  58.4 2.4 gather_fusion.25
  60.8 2.4 gather_fusion.27
  64.8 1.5 gather_fusion.1
  66.3 1.5 gather_fusion.3
  67.8 1.5 gather_fusion.7
  70.6 32.8 %gather_fusion.19 = f32[4096]{0:T(1024)S(1)} fusion(f32[256,512]{1,0:T(8,128)S(1)} %fusion.115, s32[4096]{0:T(1024)S(1)} %reshape.1051), kind=kCustom, calls=%fused_computation.5.clone | custom fusion | bytes 65536 | tf_op jit(solution)/shard_map/while/body/eval_jaxpr/jit(take_along_axis)/gather | solution.py:44
  103.7 32.8 %gather_fusion.16 = f32[4096]{0:T(1024)S(1)} fusion(f32[256,512]{1,0:T(8,128)S(1)} %fusion.112, s32[4096]{0:T(1024)S(1)} %reshape.1036), kind=kCustom, calls=%fused_computation.clone | custom fusion | bytes 65536 | tf_op jit(solution)/shard_map/while/body/eval_jaxpr/jit(take_along_axis)/gather | solution.py:44
  136.9 32.8 %gather_fusion.18 = f32[4096]{0:T(1024)S(1)} fusion(f32[256,512]{1,0:T(8,128)S(1)} %fusion.114, s32[4096]{0:T(1024)S(1)} %reshape.1046), kind=kCustom, calls=%fused_computation.4.clone | custom fusion | bytes 65536 | tf_op jit(solution)/shard_map/while/body/eval_jaxpr/jit(take_along_axis)/gather | solution.py:44
  170.1 32.8 %gather_fusion.17 = f32[4096]{0:T(1024)S(1)} fusion(f32[256,512]{1,0:T(8,128)S(1)} %fusion.113, s32[4096]{0:T(1024)S(1)} %reshape.1041), kind=kCustom, calls=%fused_computation.3.clone | custom fusion | bytes 65536 | tf_op jit(solution)/shard_map/while/body/eval_jaxpr/jit(take_along_axis)/gather | solution.py:44
  203.9 0.9 gather_fusion.5
  204.7 18.3 %all-reduce.2.cloned.1.call-done = f32[4,256,16]{1,2,0:T(8,128)} async-done(((f32[4,256,16]{1,2,0:T(8,128)}), f32[4,256,16]{1,2,0:T(8,128)}) %all-reduce.2.cloned.1.call-update) | async-done | bytes 65552 | tf_op jit(solution)/shard_map/psum | solution.py:125
  223.0 0.8 fusion.63
  223.9 2.4 gather_fusion.20
  226.3 2.4 gather_fusion.22
  228.7 2.4 gather_fusion.26
  231.1 2.4 gather_fusion.24
  234.6 6.8 %all-to-all-start.3 = ((bf16[4,16,16]{2,0,1:T(4,128)(2,1)}), bf16[4,16,16]{2,0,1:T(4,128)(2,1)S(1)}, u32[]{:S(2)}, u32[]{:S(2)}) async-start(bf16[4,16,16]{2,0,1:T(4,128)(2,1)} %pad_maximum_fusion.4), calls=%async_computation.3 | async-start | bytes 32768 | tf_op jit(solution)/shard_map/all_to_all | solution.py:141
  241.8 28.9 %scatter_custom_fusion.8 = f32[512]{0:T(512)S(1)} fusion(s32[4096]{0:T(1024)} %bitcast.383, f32[4096]{0:T(1024)S(1)} %fusion.38, f32[]{:T(128)} %constant.66.clone.1), kind=kCustom, calls=%fused_computation.287 | custom fusion | flops 4096 | bytes 2560 | tf_op jit(solution)/shard_map/scatter-max | solution.py:66
  270.7 2.1 gather_fusion
  274.4 28.9 %scatter_custom_fusion.11 = f32[512]{0:T(512)S(1)} fusion(s32[4096]{0:T(1024)} %bitcast.382, f32[4096]{0:T(1024)S(1)} %fusion.47, f32[]{:T(128)} %constant.66.clone.1), kind=kCustom, calls=%fused_computation.281 | custom fusion | flops 4096 | bytes 2560 | tf_op jit(solution)/shard_map/scatter-max | solution.py:66
  303.3 2.1 gather_fusion.6
  306.5 28.9 %scatter_custom_fusion.10 = f32[512]{0:T(512)S(1)} fusion(s32[4096]{0:T(1024)} %bitcast.381, f32[4096]{0:T(1024)S(1)} %fusion.44, f32[]{:T(128)} %constant.66.clone.1), kind=kCustom, calls=%fused_computation.283 | custom fusion | flops 4096 | bytes 2560 | tf_op jit(solution)/shard_map/scatter-max | solution.py:66
  335.5 1.9 gather_fusion.4
  338.6 28.9 %scatter_custom_fusion.9 = f32[512]{0:T(512)S(1)} fusion(s32[4096]{0:T(1024)} %bitcast.380, f32[4096]{0:T(1024)S(1)} %fusion.41, f32[]{:T(128)} %constant.66.clone.1), kind=kCustom, calls=%fused_computation.285 | custom fusion | flops 4096 | bytes 2560 | tf_op jit(solution)/shard_map/scatter-max | solution.py:66
  367.5 2.1 gather_fusion.2
  371.6 6.9 %all-to-all-start.2 = ((bf16[4,16,16,128]{3,2,0,1:T(8,128)(2,1)}), bf16[4,16,16,128]{3,2,0,1:T(8,128)(2,1)S(1)}, u32[]{:S(2)}, u32[]{:S(2)}) async-start(bf16[4,16,16,128]{3,2,0,1:T(8,128)(2,1)} %pad_maximum_fusion.1), calls=%async_computation.2 | async-start | bytes 524288 | tf_op jit(solution)/shard_map/all_to_all | solution.py:140
  379.0 1.4 gather_fusion.12
  380.3 1.2 gather_fusion.15
  381.6 1.2 gather_fusion.14
  382.8 1.4 gather_fusion.13
  384.8 3.4 all-to-all-done.2
  388.3 1.0 gather_fusion.8
  (295 shorter events, 36.6 us)
Async XLA Ops:
  12.8 17.6 %copy-start.56 = (s32[128]{0:T(128)}, s32[128]{0:T(128)S(1)}, u32[]{:S(2)}) copy-start(s32[128]{0:T(128)S(1)} %get-tuple-element.152) | copy-start | bytes 1540
  12.8 18.5 %copy-start.54 = (s32[128]{0:T(128)}, s32[128]{0:T(128)S(1)}, u32[]{:S(2)}) copy-start(s32[128]{0:T(128)S(1)} %get-tuple-element.151) | copy-start | bytes 1540
  17.9 9.6 %copy-start.24 = (s32[4,128]{1,0:T(4,128)S(1)}, s32[4,128]{1,0:T(4,128)}, u32[]{:S(2)}) copy-start(s32[4,128]{1,0:T(4,128)} %param.14) | copy-start | bytes 6148
  17.9 10.2 %copy-start.13 = (bf16[4,512,128]{2,1,0:T(8,128)(2,1)S(1)}, bf16[4,512,128]{2,1,0:T(8,128)(2,1)}, u32[]{:S(2)}) copy-start(bf16[4,512,128]{2,1,0:T(8,128)(2,1)} %param.19) | copy-start | bytes 1572868
  19.1 10.4 %copy-start.14 = (bf16[4,128,128]{2,1,0:T(8,128)(2,1)S(1)}, bf16[4,128,128]{2,1,0:T(8,128)(2,1)}, u32[]{:S(2)}) copy-start(bf16[4,128,128]{2,1,0:T(8,128)(2,1)} %param.13) | copy-start | bytes 393220
  19.1 16.1 %all-to-all-start.1 = ((s32[16,1,1216]{2,1,0:T(1,128)}), s32[16,1,1216]{2,1,0:T(1,128)S(1)}, u32[]{:S(2)}, u32[]{:S(2)}) async-start(s32[16,1,1216]{2,1,0:T(1,128)} %reshape.1189), calls=%async_computation.1 | async-start | bytes 163840 | tf_op jit(solution)/shard_map/all_to_all | solution.py:115
  35.2 34.7 %all-to-all-start = ((bf16[4,16,16,128]{3,2,0,1:T(8,128)(2,1)}), bf16[4,16,16,128]{3,2,0,1:T(8,128)(2,1)S(1)}, u32[]{:S(2)}, u32[]{:S(2)}) async-start(bf16[4,16,16,128]{3,2,0,1:T(8,128)(2,1)} %pad_maximum_fusion), calls=%async_computation | async-start | bytes 524288 | tf_op jit(solution)/shard_map/all_to_all | solution.py:114
  40.8 182.2 %all-reduce.2.cloned.1.call-start = ((), (), s32[]{:S(2)}) async-start(), calls=%async_computation.4 | async-start | bytes 131072 | tf_op jit(solution)/shard_map/psum | solution.py:125
  43.5 12.4 %copy-start = (s32[256,16]{0,1:T(8,128)}, s32[256,16]{0,1:T(8,128)S(1)}, u32[]{:S(2)}) copy-start(s32[256,16]{0,1:T(8,128)S(1)} %copy.129) | copy-start | bytes 49156
  47.9 19.9 %copy-start.26 = (s32[256,1]{0,1:T(1,128)}, s32[256,1]{0,1:T(1,128)S(1)}, u32[]{:S(2)}) copy-start(s32[256,1]{0,1:T(1,128)S(1)} %copy.140) | copy-start | bytes 3076
  48.0 5.4 %copy-start.38 = (s32[256,1]{0,1:T(1,128)}, s32[256,1]{0,1:T(1,128)S(1)}, u32[]{:S(2)}) copy-start(s32[256,1]{0,1:T(1,128)S(1)} %copy.141) | copy-start | bytes 3076
  49.7 6.2 %copy-start.32 = (s32[256,1]{0,1:T(1,128)}, s32[256,1]{0,1:T(1,128)S(1)}, u32[]{:S(2)}) copy-start(s32[256,1]{0,1:T(1,128)S(1)} %copy.127) | copy-start | bytes 3076
  49.8 6.1 %copy-start.40 = (s32[256,1]{0,1:T(1,128)}, s32[256,1]{0,1:T(1,128)S(1)}, u32[]{:S(2)}) copy-start(s32[256,1]{0,1:T(1,128)S(1)} %copy.132) | copy-start | bytes 3076
  51.5 17.7 %copy-start.30 = (s32[256,1]{0,1:T(1,128)}, s32[256,1]{0,1:T(1,128)S(1)}, u32[]{:S(2)}) copy-start(s32[256,1]{0,1:T(1,128)S(1)} %copy.137) | copy-start | bytes 3076
  51.6 4.3 %copy-start.42 = (s32[256,1]{0,1:T(1,128)}, s32[256,1]{0,1:T(1,128)S(1)}, u32[]{:S(2)}) copy-start(s32[256,1]{0,1:T(1,128)S(1)} %copy.138) | copy-start | bytes 3076
  53.4 5.0 %copy-start.28 = (s32[256,1]{0,1:T(1,128)}, s32[256,1]{0,1:T(1,128)S(1)}, u32[]{:S(2)}) copy-start(s32[256,1]{0,1:T(1,128)S(1)} %copy.134) | copy-start | bytes 3076
  53.5 10.5 %copy-start.44 = (s32[256,1]{0,1:T(1,128)}, s32[256,1]{0,1:T(1,128)S(1)}, u32[]{:S(2)}) copy-start(s32[256,1]{0,1:T(1,128)S(1)} %copy.135) | copy-start | bytes 3076
  53.5 4.8 %copy-start.2 = (s32[256,1]{0,1:T(1,128)}, s32[256,1]{0,1:T(1,128)S(1)}, u32[]{:S(2)}) copy-start(s32[256,1]{0,1:T(1,128)S(1)} %fusion.94) | copy-start | bytes 3076
  56.0 4.8 %copy-start.6 = (s32[256,1]{0,1:T(1,128)}, s32[256,1]{0,1:T(1,128)S(1)}, u32[]{:S(2)}) copy-start(s32[256,1]{0,1:T(1,128)S(1)} %fusion.91) | copy-start | bytes 3076
  58.4 4.8 %copy-start.4 = (s32[256,1]{0,1:T(1,128)}, s32[256,1]{0,1:T(1,128)S(1)}, u32[]{:S(2)}) copy-start(s32[256,1]{0,1:T(1,128)S(1)} %fusion.88) | copy-start | bytes 3076
  60.8 3.3 copy-start.8
  63.2 4.5 %copy-start.46 = (s32[1024]{0:T(1024)}, s32[1024]{0:T(1024)S(1)}, u32[]{:S(2)}) copy-start(s32[1024]{0:T(1024)S(1)} %pad_clamp_fusion.6) | copy-start | bytes 12292
  63.3 4.5 %copy-start.48 = (s32[1024]{0:T(1024)}, s32[1024]{0:T(1024)S(1)}, u32[]{:S(2)}) copy-start(s32[1024]{0:T(1024)S(1)} %pad_clamp_fusion.7) | copy-start | bytes 12292
  170.1 33.0 %copy-start.1 = (s32[256,16]{0,1:T(8,128)S(1)}, s32[256,16]{0,1:T(8,128)}, u32[]{:S(2)}) copy-start(s32[256,16]{0,1:T(8,128)} %copy-done) | copy-start | bytes 49156
  170.1 33.7 %copy-start.49 = (s32[256,1]{0,1:T(1,128)S(1)}, s32[256,1]{0,1:T(1,128)}, u32[]{:S(2)}) copy-start(s32[256,1]{0,1:T(1,128)} %compare_select_fusion.21) | copy-start | bytes 3076
  202.9 20.1 %copy-start.39 = (s32[256,1]{0,1:T(1,128)S(1)}, s32[256,1]{0,1:T(1,128)}, u32[]{:S(2)}) copy-start(s32[256,1]{0,1:T(1,128)} %copy-done.38) | copy-start | bytes 3076
  202.9 20.0 %copy-start.41 = (s32[256,1]{0,1:T(1,128)S(1)}, s32[256,1]{0,1:T(1,128)}, u32[]{:S(2)}) copy-start(s32[256,1]{0,1:T(1,128)} %copy-done.40) | copy-start | bytes 3076
  203.0 20.0 %copy-start.43 = (s32[256,1]{0,1:T(1,128)S(1)}, s32[256,1]{0,1:T(1,128)}, u32[]{:S(2)}) copy-start(s32[256,1]{0,1:T(1,128)} %copy-done.42) | copy-start | bytes 3076
  203.0 20.0 %copy-start.45 = (s32[256,1]{0,1:T(1,128)S(1)}, s32[256,1]{0,1:T(1,128)}, u32[]{:S(2)}) copy-start(s32[256,1]{0,1:T(1,128)} %copy-done.44) | copy-start | bytes 3076
  203.0 20.9 %copy-start.3 = (s32[256,1]{0,1:T(1,128)S(1)}, s32[256,1]{0,1:T(1,128)}, u32[]{:S(2)}) copy-start(s32[256,1]{0,1:T(1,128)} %copy-done.2) | copy-start | bytes 3076
  231.1 10.4 %copy-start.16 = (f32[4,256,16]{1,2,0:T(8,128)S(1)}, f32[4,256,16]{1,2,0:T(8,128)}, u32[]{:S(2)}) copy-start(f32[4,256,16]{1,2,0:T(8,128)} %all-reduce.2.cloned.1.call-done) | copy-start | bytes 196612
  231.1 10.6 %copy-start.37 = (pred[4096]{0:T(1024)(128)(4,1)S(1)}, pred[4096]{0:T(1024)(128)(4,1)}, u32[]{:S(2)}) copy-start(pred[4096]{0:T(1024)(128)(4,1)} %and.77) | copy-start | bytes 12292
  234.6 136.9 %all-to-all-start.3 = ((bf16[4,16,16]{2,0,1:T(4,128)(2,1)}), bf16[4,16,16]{2,0,1:T(4,128)(2,1)S(1)}, u32[]{:S(2)}, u32[]{:S(2)}) async-start(bf16[4,16,16]{2,0,1:T(4,128)(2,1)} %pad_maximum_fusion.4), calls=%async_computation.3 | async-start | bytes 32768 | tf_op jit(solution)/shard_map/all_to_all | solution.py:141
  241.6 31.7 %copy-start.33 = (s32[256,1]{0,1:T(1,128)S(1)}, s32[256,1]{0,1:T(1,128)}, u32[]{:S(2)}) copy-start(s32[256,1]{0,1:T(1,128)} %copy-done.32) | copy-start | bytes 3076
  270.7 3.7 copy-start.34
  274.3 31.2 %copy-start.27 = (s32[256,1]{0,1:T(1,128)S(1)}, s32[256,1]{0,1:T(1,128)}, u32[]{:S(2)}) copy-start(s32[256,1]{0,1:T(1,128)} %copy-done.26) | copy-start | bytes 3076
  306.4 31.1 %copy-start.31 = (s32[256,1]{0,1:T(1,128)S(1)}, s32[256,1]{0,1:T(1,128)}, u32[]{:S(2)}) copy-start(s32[256,1]{0,1:T(1,128)} %copy-done.30) | copy-start | bytes 3076
  338.4 31.2 %copy-start.29 = (s32[256,1]{0,1:T(1,128)S(1)}, s32[256,1]{0,1:T(1,128)}, u32[]{:S(2)}) copy-start(s32[256,1]{0,1:T(1,128)} %copy-done.28) | copy-start | bytes 3076
  338.4 32.0 %copy-start.12 = (bf16[4,16,16,128]{3,2,0,1:T(8,128)(2,1)S(1)}, bf16[4,16,16,128]{3,2,0,1:T(8,128)(2,1)}, u32[]{:S(2)}) copy-start(bf16[4,16,16,128]{3,2,0,1:T(8,128)(2,1)} %copy-done.11) | copy-start | bytes 786436
  338.4 32.0 %copy-start.17 = (bf16[256,128]{1,0:T(8,128)(2,1)S(1)}, bf16[256,128]{1,0:T(8,128)(2,1)}, u32[]{:S(2)}) copy-start(bf16[256,128]{1,0:T(8,128)(2,1)} %gather_fusion.1) | copy-start | bytes 196612
  338.4 32.0 %copy-start.18 = (bf16[256,128]{1,0:T(8,128)(2,1)S(1)}, bf16[256,128]{1,0:T(8,128)(2,1)}, u32[]{:S(2)}) copy-start(bf16[256,128]{1,0:T(8,128)(2,1)} %gather_fusion.3) | copy-start | bytes 196612
  338.4 32.0 %copy-start.19 = (bf16[256,128]{1,0:T(8,128)(2,1)S(1)}, bf16[256,128]{1,0:T(8,128)(2,1)}, u32[]{:S(2)}) copy-start(bf16[256,128]{1,0:T(8,128)(2,1)} %gather_fusion.7) | copy-start | bytes 196612
  370.8 7.7 %copy-start.55 = (s32[128]{0:T(128)S(1)}, s32[128]{0:T(128)}, u32[]{:S(2)}) copy-start(s32[128]{0:T(128)} %copy-done.54) | copy-start | bytes 1540
  370.8 7.7 %copy-start.57 = (s32[128]{0:T(128)S(1)}, s32[128]{0:T(128)}, u32[]{:S(2)}) copy-start(s32[128]{0:T(128)} %copy-done.56) | copy-start | bytes 1540
  371.6 16.6 %all-to-all-start.2 = ((bf16[4,16,16,128]{3,2,0,1:T(8,128)(2,1)}), bf16[4,16,16,128]{3,2,0,1:T(8,128)(2,1)S(1)}, u32[]{:S(2)}, u32[]{:S(2)}) async-start(bf16[4,16,16,128]{3,2,0,1:T(8,128)(2,1)} %pad_maximum_fusion.1), calls=%async_computation.2 | async-start | bytes 524288 | tf_op jit(solution)/shard_map/all_to_all | solution.py:140
  388.2 3.3 copy-start.15
  388.2 3.3 copy-start.50
  388.3 3.3 copy-start.51
  (15 other events, 37.7 us)
Sparse Core Ops, SparseCore 0:
  203.9 18.9 all-reduce.1
where the time goes:
time: 400 us; the launch traced here: 399 us
  local copies, waits for them, and re-layouts  201 us (50%)
  other arithmetic  130 us (32%)
  starting transfers between devices  28 us (7%)
  waiting for transfers between devices  23 us (6%)
  between operations  15.6 us (4%)
    gather x20, local copies, waits for them, and re-layouts, score_block(): return jnp.take_along_axis(tile_scores, index_block, axis=1)  132 us
    another operation x4, other arithmetic, settle_requests(): claims = jnp.zeros((desc_table.shape[0],), jnp.float32).at[listed.reshape...  116 us
    psum x1, waiting for transfers between devices, body(): summed_all = lax.psum(partial_all, 'rep')  18.3 us
    gather x4, local copies, waits for them, and re-layouts, settle_requests(): chosen_quality = jnp.take_along_axis(quality, pick_pos, 1)[:, 0]  9.48 us
    gather x4, local copies, waits for them, and re-layouts, settle_requests(): chosen = jnp.take_along_axis(listed, pick_pos, 1)[:, 0]  9.48 us
    all_to_all x1, starting transfers between devices, body(): lax.all_to_all(all_meta, 'space', split_axis=1, concat_axis=1, tiled=True)  8.47 us
    gather x4, local copies, waits for them, and re-layouts, settle_requests(): share_weight = chosen_quality / (chosen_quality + claims[chosen])  8.19 us
  transfers between devices with their start and end apart: 5, of which 3 were waited for; matrix products, arithmetic and copies ran while one was open for 43% of the time, Pallas kernels for 0%

commit v1 on v0

v1 whole, which is shorter than its diff:
```python
import functools
import math

import jax
import jax.numpy as jnp
from jax import lax
from jax.experimental import pallas as pl
from jax.experimental.pallas import tpu as pltpu
from jax.sharding import PartitionSpec as P

MESH = pl.DeviceIdType.MESH
F32 = jnp.float32
BF16 = jnp.bfloat16
NEG = -1e30
GROUP = 32
NT = (((1,), (1,)), ((), ()))
TN = (((0,), (0,)), ((), ()))


def iota(shape, dim):
    return lax.broadcasted_iota(jnp.int32, shape, dim)


def dot(a, b):
    return jnp.dot(a, b, preferred_element_type=F32)


def hot(mask):
    return jnp.where(mask, 1.0, 0.0).astype(BF16)


def code(index, cands):
    return index - cands // 2 + jnp.where(index >= cands // 2, 1, 0)


def kernel(
    n, slots, width,
    halo, unmatched, owner, cand, lengths, choice, desc,
    phantom, best,
    send, recv, send_meta, recv_meta, table, scores, back, recv_back, back_best, recv_best,
    row_ss, row_rs, meta_ss, meta_rs, back_ss, back_rs, best_ss, best_rs, table_sem, local_sem,
):
    me, core = lax.axis_index("space"), lax.axis_index("rep")
    snaps, halos, half = halo.shape
    k_count = cand.shape[1]
    cands = desc.shape[1]
    own = snaps // 2
    total = n * slots

    def core_of(x):
        return lax.rem(core + x, 2)

    def remote(src, dst, ss, rs, peer, x):
        return pltpu.make_async_remote_copy(
            src_ref=src, dst_ref=dst, send_sem=ss, recv_sem=rs,
            device_id=(peer, core_of(x)), device_id_type=MESH,
        )

    def each_peer(f):
        @pl.loop(1, n)
        def _(d):
            peer = lax.rem(me + d, n)
            f(peer, 0)
            f(peer, 1)

        f(me, 1)

    def each_chip(f):
        @pl.loop(1, n)
        def _(d):
            f(lax.rem(me + d, n))

    barrier = pltpu.get_barrier_semaphore()
    each_peer(
        lambda peer, x: pl.semaphore_signal(
            barrier, inc=1, device_id=(peer, core_of(x)), device_id_type=MESH
        )
    )

    upper = hot(iota((halos, halos), 0) < iota((halos, halos), 1))
    route = []
    for x in range(2):
        for ls in range(own):
            s = own * core_of(x) + ls
            dest = owner[s]
            named = iota((n, halos), 0) == dest
            onehot = hot(named)
            rank = jnp.sum(jnp.where(named, dot(onehot, upper), 0.0), axis=0, keepdims=True)
            rank = rank.astype(jnp.int32)
            live = unmatched[pl.ds(s, 1), :] == 1
            target = jnp.where(live, dest * slots + rank, -1)
            route.append((onehot, rank, target, live))

    meta = None
    for x in range(2):
        for ls in range(own):
            s = own * core_of(x) + ls
            _, _, target, live = route[x * own + ls]
            place = hot(iota((total, halos), 0) == target)
            rows = dot(place, halo[s]).astype(BF16)
            send[x, :, ls * slots : (ls + 1) * slots, :] = rows.reshape(n, slots, half)
            if x == 0:
                listed = code(cand[s], cands)
                k_ids = iota((k_count, halos), 0)
                pick = jnp.sum(
                    jnp.where(k_ids == choice[pl.ds(s, 1), :], listed, 0), axis=0, keepdims=True
                )
                listed = jnp.where(k_ids < lengths[pl.ds(s, 1), :], listed, 0)
                block = jnp.concatenate(
                    [listed, jnp.broadcast_to(pick, (GROUP - k_count, halos))], axis=0
                ).astype(F32)
                parts = [block]
                if ls > 0:
                    parts.insert(0, jnp.zeros((ls * GROUP, halos), F32))
                parts.append(jnp.zeros((128 - (ls + 1) * GROUP, halos), F32))
                block = jnp.concatenate(parts, axis=0).astype(BF16)
                term = lax.dot_general(place, block, NT, preferred_element_type=F32)
                meta = term if meta is None else meta + term
    send_meta[...] = meta.astype(BF16).reshape(n, slots, 128)

    pl.semaphore_wait(barrier, 2 * n - 1)

    def row_copy(peer, x):
        return remote(send.at[x, peer], recv.at[x, me], row_ss.at[x, peer], row_rs.at[x, me], peer, x)

    def row_arrival(peer, x):
        return remote(send.at[x, peer], recv.at[x, peer], row_ss.at[x, peer], row_rs.at[x, peer], peer, x)

    def meta_copy(peer):
        return remote(send_meta.at[peer], recv_meta.at[me], meta_ss.at[peer], meta_rs.at[me], peer, 0)

    def meta_arrival(peer):
        return remote(send_meta.at[peer], recv_meta.at[peer], meta_ss.at[peer], meta_rs.at[peer], peer, 0)

    each_chip(lambda peer: meta_copy(peer).start())
    each_peer(lambda peer, x: row_copy(peer, x).start())
    table_copy = remote(
        desc.at[pl.ds(own * core_of(1), own)], table, table_sem.at[0], table_sem.at[1], me, 1
    )
    table_copy.start()
    local_row = pltpu.make_async_copy(send.at[0, me], recv.at[0, me], local_sem.at[0])
    local_meta = pltpu.make_async_copy(send_meta.at[me], recv_meta.at[me], local_sem.at[1])
    local_row.start()
    local_meta.start()

    local_row.wait()
    local_meta.wait()
    table_copy.wait_recv()
    each_chip(lambda peer: meta_arrival(peer).wait_recv())
    each_peer(lambda peer, x: row_arrival(peer, x).wait_recv())

    meta_all = recv_meta[...].reshape(total, 128).astype(F32)
    meta_rows = meta_all.T
    step = 64
    fold = None
    for ls in range(own):
        s = own * core + ls
        halves = [
            recv[x, :, ls * slots : (ls + 1) * slots, :].reshape(total, half) for x in range(2)
        ]
        tables = [desc[s], table[ls]]
        scores[...] = lax.dot_general(
            jnp.concatenate(tables, axis=1), jnp.concatenate(halves, axis=1), NT,
            preferred_element_type=F32,
        )
        lists = meta_rows[ls * GROUP : ls * GROUP + k_count]
        pick = meta_rows[ls * GROUP + k_count : ls * GROUP + k_count + 1]

        def chunk(i, carry):
            top, picked, claimed = carry
            ids = code(iota((step, total), 0) + i * step, cands).astype(F32)
            value = scores[pl.ds(pl.multiple_of(i * step, step), step), :]
            mask = ids == lists[0:1]
            for k in range(1, k_count):
                mask = mask | (ids == lists[k : k + 1])
            masked = jnp.where(mask, value, NEG)
            claim = jnp.max(masked, axis=1, keepdims=True)
            chosen = ids == pick

            def least(v):
                return jnp.max(v.reshape(step // 8, 8, total), axis=0)

            return (
                jnp.maximum(top, least(masked)),
                jnp.maximum(picked, least(jnp.where(chosen, value, NEG))),
                jnp.maximum(claimed, least(jnp.where(chosen, claim, NEG))),
            )

        start = jnp.full((8, total), NEG, F32)
        top, picked, claimed = [
            jnp.max(v, axis=0, keepdims=True)
            for v in lax.fori_loop(0, cands // step, chunk, (start, start, start))
        ]

        def quality(v):
            v = v * (1.0 / math.sqrt(width))
            return 1.0 + jnp.maximum(v, 0.0) + jnp.log(1.0 + jnp.exp(-jnp.abs(v)))

        mine = quality(picked)
        share = mine / (mine + quality(claimed))
        share = jnp.broadcast_to(share, (128, total)).T
        column = meta_all[:, ls * GROUP + k_count : ls * GROUP + k_count + 1]
        select = hot(column == code(iota((total, cands), 1), cands).astype(F32))
        for x in range(2):
            taken = dot(select, tables[x])
            blend = (1.0 - share) * halves[x].astype(F32) + share * taken
            back[x, :, ls * slots : (ls + 1) * slots, :] = blend.astype(BF16).reshape(n, slots, half)

        top = jnp.where(top > NEG * 0.5, top * (1.0 / math.sqrt(width)), 0.0)
        spread = jnp.where(
            iota((n, total), 0) == iota((n, total), 1) // slots, jnp.broadcast_to(top, (n, total)), 0.0
        ).astype(BF16)
        lane = iota((total, 128), 0)
        term = dot(spread, hot(iota((total, 128), 1) == ls * slots + lane % slots))
        fold = term if fold is None else fold + term
    back_best[...] = fold.reshape(n, 1, 128)

    def back_copy(peer, x):
        return remote(back.at[x, peer], recv_back.at[x, me], back_ss.at[x, peer], back_rs.at[x, me], peer, x)

    def back_arrival(peer, x):
        return remote(back.at[x, peer], recv_back.at[x, peer], back_ss.at[x, peer], back_rs.at[x, peer], peer, x)

    def best_copy(peer, x):
        return remote(back_best.at[peer], recv_best.at[x, me], best_ss.at[x, peer], best_rs.at[x, me], peer, x)

    def best_arrival(peer, x):
        return remote(back_best.at[peer], recv_best.at[x, peer], best_ss.at[x, peer], best_rs.at[x, peer], peer, x)

    each_peer(lambda peer, x: back_copy(peer, x).start())
    each_peer(lambda peer, x: best_copy(peer, x).start())
    local_back = pltpu.make_async_copy(back.at[0, me], recv_back.at[0, me], local_sem.at[2])
    local_best = pltpu.make_async_copy(back_best.at[me], recv_best.at[0, me], local_sem.at[3])
    local_back.start()
    local_best.start()
    local_back.wait()
    local_best.wait()
    each_peer(lambda peer, x: back_arrival(peer, x).wait_recv())
    each_peer(lambda peer, x: best_arrival(peer, x).wait_recv())

    tops = []
    for x in range(2):
        brought = recv_best[x].reshape(n, 128).astype(BF16)
        for ls in range(own):
            s = own * core_of(x) + ls
            onehot, rank, target, live = route[x * own + ls]
            column = jnp.broadcast_to(target.astype(F32), (128, halos)).T[:, 0:1]
            place = hot(iota((halos, total), 1).astype(F32) == column)
            rows = dot(place, recv_back[x, :, ls * slots : (ls + 1) * slots, :].reshape(total, half))
            phantom[s] = jnp.where(column < 0.0, halo[s].astype(F32), rows).astype(BF16)
            spread = lax.dot_general(brought, onehot, TN, preferred_element_type=F32)
            here = jnp.where(iota((128, halos), 0) == ls * slots + rank, spread, 0.0)
            tops.append(jnp.where(live, jnp.sum(here, axis=0, keepdims=True), 0.0))
    first, second = jnp.concatenate(tops[:own], axis=0), jnp.concatenate(tops[own:], axis=0)
    even = core == 0
    best[...] = jnp.concatenate(
        [jnp.where(even, first, second), jnp.where(even, second, first)], axis=0
    ).astype(BF16)

    table_copy.wait_send()
    each_chip(lambda peer: meta_copy(peer).wait_send())
    each_peer(lambda peer, x: row_copy(peer, x).wait_send())
    each_peer(lambda peer, x: back_copy(peer, x).wait_send())
    each_peer(lambda peer, x: best_copy(peer, x).wait_send())


def body(n, halo_rows, unmatched, owner_id, cand_index, lengths, choice_index, desc_rows):
    snaps, halos, half = halo_rows.shape
    cands = desc_rows.shape[1]
    own = snaps // 2
    slots = max(2 * halos // n, 16)
    total = n * slots
    dma = pltpu.SemaphoreType.DMA
    return pl.pallas_call(
        functools.partial(kernel, n, slots, 2 * half),
        out_shape=(
            jax.ShapeDtypeStruct((snaps, halos, half), BF16),
            jax.ShapeDtypeStruct((snaps, halos), BF16),
        ),
        in_specs=[pl.BlockSpec(memory_space=pltpu.VMEM)] * 7,
        out_specs=(pl.BlockSpec(memory_space=pltpu.VMEM),) * 2,
        scratch_shapes=[
            pltpu.VMEM((2, n, own * slots, half), BF16),
            pltpu.VMEM((2, n, own * slots, half), BF16),
            pltpu.VMEM((n, slots, 128), BF16),
            pltpu.VMEM((n, slots, 128), BF16),
            pltpu.VMEM((own, cands, half), BF16),
            pltpu.VMEM((cands, total), F32),
            pltpu.VMEM((2, n, own * slots, half), BF16),
            pltpu.VMEM((2, n, own * slots, half), BF16),
            pltpu.VMEM((n, 1, 128), F32),
            pltpu.VMEM((2, n, 1, 128), F32),
            dma((2, n)), dma((2, n)), dma((n,)), dma((n,)),
            dma((2, n)), dma((2, n)), dma((2, n)), dma((2, n)),
            dma((2,)), dma((4,)),
        ],
        compiler_params=pltpu.CompilerParams(collective_id=0, has_side_effects=True),
    )(
        halo_rows,
        unmatched,
        jnp.swapaxes(owner_id, 1, 2),
        jnp.swapaxes(cand_index, 1, 2),
        lengths,
        choice_index,
        desc_rows,
    )


def solution(mesh):
    in_specs = (
        P(None, "space", "rep"),
        P(None, "space"),
        P(None, "space", None),
        P(None, "space", None),
        P(None, "space"),
        P(None, "space"),
        P(None, "space", "rep"),
    )
    out_specs = (P(None, "space", "rep"), P(None, "space"))
    return jax.shard_map(
        functools.partial(body, mesh.shape["space"]),
        mesh=mesh, in_specs=in_specs, out_specs=out_specs, check_vma=False,
    )
```

time: 400 us -> 37.7 us (0.09)
  local copies, waits for them, and re-layouts: 201 us -> 2.14 us
  other arithmetic: 130 us -> 0 us
  Pallas kernels: 0 us -> 34.7 us
  starting transfers between devices: 28 us -> 0 us
  waiting for transfers between devices: 23 us -> 0 us
  between operations: 15.6 us -> 0.65 us
    gather x44 -> x0, local copies, waits for them, and re-layouts: 173 us -> none  [the longest x20 132 us: score_block(): return jnp.take_along_axis(tile_scores, index_block, axis=1)]
    another operation x11 -> x0, other arithmetic: 120 us -> none  [the longest x4 116 us: settle_requests(): claims = jnp.zeros((desc_table.shape[0],), jnp.float32).at[listed.reshape...]
    pallas_call x0 -> x1, Pallas kernels: none -> 34.7 us  [body(): pl.pallas_call(functools.partial(kernel, n, slots, 2 * half), out_shape=(...]
    all_to_all x4 -> x0, starting transfers between devices: 27.8 us -> none  [the longest x1 8.47 us: body(): lax.all_to_all(all_meta, 'space', split_axis=1, concat_axis=1, tiled=True)]
    psum x1 -> x0, waiting for transfers between devices: 18.3 us -> none  [body(): summed_all = lax.psum(partial_all, 'rep')]
    scatter x8 -> x0, local copies, waits for them, and re-layouts: 7.27 us -> none  [the longest x4 3.65 us: route_snapshot(): jnp.zeros((slot_total, K + 3), jnp.int32).at[target].set(meta_rows)]
    all_to_all x4 -> x0, waiting for transfers between devices: 4.72 us -> none  [the longest x1 3.42 us: body(): lax.all_to_all(blended_all, 'space', split_axis=1, concat_axis=1, tiled=T...]
    select_n x15 -> x0, other arithmetic: 4.02 us -> none  [the longest x4 2.46 us: settle_requests(): claims = jnp.zeros((desc_table.shape[0],), jnp.float32).at[listed.reshape...]
  transfers between devices with their start and end apart: 5 -> 0, of which waited for: 3 -> 0; matrix products, arithmetic and copies ran while one was open for 43% -> 0% of each run, Pallas kernels for 0% -> 0%
where the time goes in v1:
time: 37.7 us; the launch traced here: 37.5 us
  Pallas kernels  34.7 us (92%)
  local copies, waits for them, and re-layouts  2.14 us (6%)
  between operations  0.65 us (2%)
    pallas_call x1, Pallas kernels, body(): pl.pallas_call(functools.partial(kernel, n, slots, 2 * half), out_shape=(...  34.7 us
    unnamed x4, local copies, waits for them, and re-layouts  2.14 us

profile of v1, /device:TPU:0, one launch (start us, length us, event | category | flops | bytes accessed | tf_op | source)
XLA Modules:
  0.0 37.5 jit_solution(14672909919673119731)
XLA Ops:
  0.6 34.7 %shard_map.86 = (bf16[4,128,128]{2,1,0:T(8,128)(2,1)}, bf16[4,128]{1,0:T(4,128)(2,1)}) custom-call(bf16[4,128,128]{2,1,0:T(8,128)(2,1)} %halo.1, s32[4,128]{1,0:T(4,128)} %unmatched.1, s32[4,1,128]{2,1,0:T(1,128)} %bitcast.3, s32[4,16,128]{2,1,0:T(8,128)} %bitcast.2, s32[4,128]{1,0:T(4,128)} %lengths.1, s32[4,128]{1,0:T(4,128)} %choice.1, ...), custom_call_target="tpu_custom_call" | custom-call | tf_op jit(solution)/shard_map/pallas_call | solution.py:274
  35.4 0.0 copy-start
  35.4 1.6 %copy.11 = bf16[4,128,128]{2,1,0:T(8,128)(2,1)} copy(bf16[4,128,128]{2,1,0:T(8,128)(2,1)} %get-tuple-element.4) | data formatting | bytes 262144
  37.0 0.0 copy-done
  37.0 0.6 %copy.12 = bf16[4,128]{1,0:T(4,128)(2,1)} copy(bf16[4,128]{1,0:T(4,128)(2,1)S(1)} %copy-done) | data formatting | bytes 2048
Async XLA Ops:
  35.4 1.6 %copy-start = (bf16[4,128]{1,0:T(4,128)(2,1)S(1)}, bf16[4,128]{1,0:T(4,128)(2,1)}, u32[]{:S(2)}) copy-start(bf16[4,128]{1,0:T(4,128)(2,1)} %get-tuple-element.5) | copy-start | bytes 3076

commit v2 on v1

v2 whole, which is shorter than its diff:
```python
import functools
import math

import jax
import jax.numpy as jnp
from jax import lax
from jax.experimental import pallas as pl
from jax.experimental.pallas import tpu as pltpu
from jax.sharding import PartitionSpec as P

MESH = pl.DeviceIdType.MESH
F32 = jnp.float32
BF16 = jnp.bfloat16
NEG = -1e30
GROUP = 32
NT = (((1,), (1,)), ((), ()))
TN = (((0,), (0,)), ((), ()))


def iota(shape, dim):
    return lax.broadcasted_iota(jnp.int32, shape, dim)


def dot(a, b):
    return jnp.dot(a, b, preferred_element_type=F32)


def hot(mask):
    return jnp.where(mask, 1.0, 0.0).astype(BF16)


def code(index, cands):
    return index - cands // 2 + jnp.where(index >= cands // 2, 1, 0)


def kernel(
    n, slots, width,
    halo, unmatched, owner, cand, lengths, choice, desc,
    phantom, best,
    send, recv, send_meta, recv_meta, mine_table, table, scores, bias, taken,
    back, recv_back, back_best, recv_best,
    row_ss, row_rs, meta_ss, meta_rs, back_ss, back_rs, best_ss, best_rs, table_sem, local_sem,
):
    me, core = lax.axis_index("space"), lax.axis_index("rep")
    snaps, halos, half = halo.shape
    k_count = cand.shape[1]
    cands = desc.shape[1]
    own = snaps // 2
    total = n * slots
    hs = slots // 2

    def core_of(x):
        return lax.rem(core + x, 2)

    def remote(src, dst, ss, rs, peer, x):
        return pltpu.make_async_remote_copy(
            src_ref=src, dst_ref=dst, send_sem=ss, recv_sem=rs,
            device_id=(peer, core_of(x)), device_id_type=MESH,
        )

    bits = n.bit_length() - 1
    mine_bits = [lax.rem(lax.div(me, 1 << i), 2) for i in range(bits)]

    def far_first(f):
        @pl.loop(1, n)
        def _(d):
            if n == 1 << bits:
                m = n - d
                peer = 0
                for i in range(bits):
                    flip = lax.rem(lax.div(m, 1 << i), 2)
                    peer = peer + (mine_bits[i] + flip - 2 * mine_bits[i] * flip) * (1 << i)
            else:
                peer = lax.rem(me + d, n)
            f(peer)

    def each_chip(f):
        @pl.loop(1, n)
        def _(d):
            f(lax.rem(me + d, n))

    def each_peer(f, order=each_chip):
        def both(peer):
            f(peer, 0)
            f(peer, 1)

        order(both)
        f(me, 1)

    barrier = pltpu.get_barrier_semaphore()
    each_peer(
        lambda peer, x: pl.semaphore_signal(
            barrier, inc=1, device_id=(peer, core_of(x)), device_id_type=MESH
        ),
        far_first,
    )
    own_table = pltpu.make_async_copy(desc.at[pl.ds(own * core, own)], mine_table, local_sem.at[0])
    own_table.start()

    upper = hot(iota((halos, halos), 0) < iota((halos, halos), 1))
    route = []
    for x in range(2):
        for ls in range(own):
            s = own * core_of(x) + ls
            dest = owner[s]
            named = iota((n, halos), 0) == dest
            onehot = hot(named)
            rank = jnp.sum(jnp.where(named, dot(onehot, upper), 0.0), axis=0, keepdims=True)
            rank = rank.astype(jnp.int32)
            live = unmatched[pl.ds(s, 1), :] == 1
            target = jnp.where(live, dest * slots + rank, -1)
            route.append((onehot, rank, target, live))

    meta = None
    for ls in range(own):
        s = own * core + ls
        _, rank, _, live = route[ls]
        listed = code(cand[s], cands)
        k_ids = iota((k_count, halos), 0)
        pick = jnp.sum(jnp.where(k_ids == choice[pl.ds(s, 1), :], listed, 0), axis=0, keepdims=True)
        listed = jnp.where(k_ids < lengths[pl.ds(s, 1), :], listed, 0)
        block = jnp.concatenate(
            [listed, jnp.broadcast_to(pick, (GROUP - k_count, halos))], axis=0
        ).astype(F32)
        for g in range(2):
            lead = (g * own + ls) * GROUP
            parts = [jnp.zeros((lead, halos), F32)] if lead else []
            parts.append(block)
            if lead + GROUP < 128:
                parts.append(jnp.zeros((128 - lead - GROUP, halos), F32))
            here = live & (rank >= g * hs) & (rank < (g + 1) * hs)
            row = jnp.where(here, owner[s] * hs + rank - g * hs, -1)
            term = lax.dot_general(
                hot(iota((n * hs, halos), 0) == row),
                (jnp.concatenate(parts, axis=0) if len(parts) > 1 else block).astype(BF16),
                NT, preferred_element_type=F32,
            )
            meta = term if meta is None else meta + term
    send_meta[...] = meta.astype(BF16).reshape(n, hs, 128)

    for ls in range(own):
        for x in range(2):
            place = hot(iota((total, halos), 0) == route[x * own + ls][2])
            rows = dot(place, halo[own * core_of(x) + ls]).astype(BF16)
            send[ls, x] = rows.reshape(n, slots, half)

    pl.semaphore_wait(barrier, 2 * n - 1)

    def row_copy(ls, peer, x, at):
        return remote(
            send.at[ls, x, peer], recv.at[ls, x, at], row_ss.at[ls, x, peer], row_rs.at[ls, x, at], peer, x
        )

    def meta_copy(peer, at):
        return remote(send_meta.at[peer], recv_meta.at[at], meta_ss.at[peer], meta_rs.at[at], peer, 0)

    table_copy = remote(
        desc.at[pl.ds(own * core_of(1), own)], table, table_sem.at[0], table_sem.at[1], me, 1
    )
    table_copy.start()
    far_first(lambda peer: meta_copy(peer, me).start())
    for ls in range(own):
        each_peer(lambda peer, x: row_copy(ls, peer, x, me).start(), far_first)
    local_meta = pltpu.make_async_copy(send_meta.at[me], recv_meta.at[me], local_sem.at[1])
    local_meta.start()
    local_rows = []
    for ls in range(own):
        local_rows.append(
            pltpu.make_async_copy(send.at[ls, 0, me], recv.at[ls, 0, me], local_sem.at[2 + ls])
        )
        local_rows[-1].start()

    step = 64
    entry = iota((n * hs, total), 0)
    column = iota((n * hs, total), 1)
    inside = column % slots
    unpack = [
        hot((entry == (column // slots) * hs + inside - g * hs) & (inside // hs == g)) for g in range(2)
    ]
    local_meta.wait()
    each_chip(lambda peer: meta_copy(peer, peer).wait_recv())
    arrived = recv_meta[...].reshape(n * hs, 128).astype(F32).T.astype(BF16)
    picks = []
    for ls in range(own):
        lists = sum(
            dot(arrived[(g * own + ls) * GROUP : (g * own + ls + 1) * GROUP], unpack[g]) for g in range(2)
        )
        picks.append(lists[k_count : k_count + 1])

        @pl.loop(0, cands // step)
        def _(i):
            ids = code(iota((step, total), 0) + i * step, cands).astype(F32)
            mask = ids == lists[0:1]
            for k in range(1, k_count):
                mask = mask | (ids == lists[k : k + 1])
            bias[ls, pl.ds(pl.multiple_of(i * step, step), step), :] = jnp.where(mask, 0.0, NEG)

    own_table.wait()
    table_copy.wait_recv()
    for ls in range(own):
        chosen = jnp.broadcast_to(picks[ls], (128, total)).T[:, 0:1]
        select = hot(chosen == code(iota((total, cands), 1), cands).astype(F32))
        taken[ls, 0] = dot(select, mine_table[ls])
        taken[ls, 1] = dot(select, table[ls])

    def back_copy(ls, peer, x, at):
        return remote(
            back.at[ls, x, peer], recv_back.at[ls, x, at],
            back_ss.at[ls, x, peer], back_rs.at[ls, x, at], peer, x,
        )

    def best_copy(peer, x, at):
        return remote(back_best.at[peer], recv_best.at[x, at], best_ss.at[x, peer], best_rs.at[x, at], peer, x)

    scale = 1.0 / math.sqrt(width)
    lane = iota((total, 128), 0)
    fold = None
    local_backs = []
    for ls in range(own):
        local_rows[ls].wait()
        each_peer(lambda peer, x: row_copy(ls, peer, x, peer).wait_recv())
        halves = [recv[ls, x].reshape(total, half) for x in range(2)]
        scores[...] = lax.dot_general(
            jnp.concatenate([mine_table[ls], table[ls]], axis=1), jnp.concatenate(halves, axis=1), NT,
            preferred_element_type=F32,
        )

        def chunk(i, carry):
            top, picked, claimed = carry
            at = pl.ds(pl.multiple_of(i * step, step), step)
            value = scores[at, :]
            masked = value + bias[ls, at, :]
            claim = jnp.max(masked, axis=1, keepdims=True)
            chosen = code(iota((step, total), 0) + i * step, cands).astype(F32) == picks[ls]

            def least(v):
                return jnp.max(v.reshape(step // 8, 8, total), axis=0)

            return (
                jnp.maximum(top, least(masked)),
                jnp.maximum(picked, least(jnp.where(chosen, value, NEG))),
                jnp.maximum(claimed, least(jnp.where(chosen, claim, NEG))),
            )

        start = jnp.full((8, total), NEG, F32)
        top, picked, claimed = [
            jnp.max(v, axis=0, keepdims=True)
            for v in lax.fori_loop(0, cands // step, chunk, (start, start, start))
        ]

        def quality(v):
            v = v * scale
            return 1.0 + jnp.maximum(v, 0.0) + jnp.log(1.0 + jnp.exp(-jnp.abs(v)))

        mine = quality(picked)
        share = mine / (mine + quality(claimed))
        share = jnp.broadcast_to(share, (128, total)).T
        for x in range(2):
            blend = (1.0 - share) * halves[x].astype(F32) + share * taken[ls, x]
            back[ls, x] = blend.astype(BF16).reshape(n, slots, half)

        top = jnp.where(top > NEG * 0.5, top * scale, 0.0)
        spread = jnp.where(
            iota((n, total), 0) == iota((n, total), 1) // slots, jnp.broadcast_to(top, (n, total)), 0.0
        ).astype(BF16)
        term = dot(spread, hot(iota((total, 128), 1) == ls * slots + lane % slots))
        fold = term if fold is None else fold + term
        if ls == own - 1:
            back_best[...] = fold.reshape(n, 1, 128)
            each_peer(lambda peer, x: best_copy(peer, x, me).start(), far_first)
        each_peer(lambda peer, x: back_copy(ls, peer, x, me).start(), far_first)
        local_backs.append(
            pltpu.make_async_copy(back.at[ls, 0, me], recv_back.at[ls, 0, me], local_sem.at[2 + own + ls])
        )
        local_backs[-1].start()
    local_best = pltpu.make_async_copy(back_best.at[me], recv_best.at[0, me], local_sem.at[2 + 2 * own])
    local_best.start()

    columns = [
        jnp.broadcast_to(target.astype(F32), (128, halos)).T[:, 0:1] for _, _, target, _ in route
    ]
    for ls in range(own):
        local_backs[ls].wait()
        each_peer(lambda peer, x: back_copy(ls, peer, x, peer).wait_recv())
        for x in range(2):
            s = own * core_of(x) + ls
            column = columns[x * own + ls]
            place = hot(iota((halos, total), 1).astype(F32) == column)
            rows = dot(place, recv_back[ls, x].reshape(total, half))
            phantom[s] = jnp.where(column < 0.0, halo[s].astype(F32), rows).astype(BF16)

    local_best.wait()
    each_peer(lambda peer, x: best_copy(peer, x, peer).wait_recv())
    tops = []
    for x in range(2):
        brought = recv_best[x].reshape(n, 128).astype(BF16)
        for ls in range(own):
            onehot, rank, _, live = route[x * own + ls]
            spread = lax.dot_general(brought, onehot, TN, preferred_element_type=F32)
            here = jnp.where(iota((128, halos), 0) == ls * slots + rank, spread, 0.0)
            tops.append(jnp.where(live, jnp.sum(here, axis=0, keepdims=True), 0.0))
    first, second = jnp.concatenate(tops[:own], axis=0), jnp.concatenate(tops[own:], axis=0)
    even = core == 0
    best[...] = jnp.concatenate(
        [jnp.where(even, first, second), jnp.where(even, second, first)], axis=0
    ).astype(BF16)

    table_copy.wait_send()
    each_chip(lambda peer: meta_copy(peer, me).wait_send())
    for ls in range(own):
        each_peer(lambda peer, x: row_copy(ls, peer, x, me).wait_send())
        each_peer(lambda peer, x: back_copy(ls, peer, x, me).wait_send())
    each_peer(lambda peer, x: best_copy(peer, x, me).wait_send())


def body(n, halo_rows, unmatched, owner_id, cand_index, lengths, choice_index, desc_rows):
    snaps, halos, half = halo_rows.shape
    cands = desc_rows.shape[1]
    own = snaps // 2
    slots = max(2 * halos // n, 16)
    total = n * slots
    dma = pltpu.SemaphoreType.DMA
    return pl.pallas_call(
        functools.partial(kernel, n, slots, 2 * half),
        out_shape=(
            jax.ShapeDtypeStruct((snaps, halos, half), BF16),
            jax.ShapeDtypeStruct((snaps, halos), BF16),
        ),
        in_specs=[pl.BlockSpec(memory_space=pltpu.VMEM)] * 6 + [pl.BlockSpec(memory_space=pl.ANY)],
        out_specs=(pl.BlockSpec(memory_space=pltpu.VMEM),) * 2,
        scratch_shapes=[
            pltpu.VMEM((own, 2, n, slots, half), BF16),
            pltpu.VMEM((own, 2, n, slots, half), BF16),
            pltpu.VMEM((n, slots // 2, 128), BF16),
            pltpu.VMEM((n, slots // 2, 128), BF16),
            pltpu.VMEM((own, cands, half), BF16),
            pltpu.VMEM((own, cands, half), BF16),
            pltpu.VMEM((cands, total), F32),
            pltpu.VMEM((own, cands, total), F32),
            pltpu.VMEM((own, 2, total, half), F32),
            pltpu.VMEM((own, 2, n, slots, half), BF16),
            pltpu.VMEM((own, 2, n, slots, half), BF16),
            pltpu.VMEM((n, 1, 128), F32),
            pltpu.VMEM((2, n, 1, 128), F32),
            dma((own, 2, n)), dma((own, 2, n)), dma((n,)), dma((n,)),
            dma((own, 2, n)), dma((own, 2, n)), dma((2, n)), dma((2, n)),
            dma((2,)), dma((3 + 2 * own,)),
        ],
        compiler_params=pltpu.CompilerParams(collective_id=0, has_side_effects=True),
    )(
        halo_rows,
        unmatched,
        jnp.swapaxes(owner_id, 1, 2),
        jnp.swapaxes(cand_index, 1, 2),
        lengths,
        choice_index,
        desc_rows,
    )


def solution(mesh):
    in_specs = (
        P(None, "space", "rep"),
        P(None, "space"),
        P(None, "space", None),
        P(None, "space", None),
        P(None, "space"),
        P(None, "space"),
        P(None, "space", "rep"),
    )
    out_specs = (P(None, "space", "rep"), P(None, "space"))
    return jax.shard_map(
        functools.partial(body, mesh.shape["space"]),
        mesh=mesh, in_specs=in_specs, out_specs=out_specs, check_vma=False,
    )
```

time: 37.7 us -> 33.6 us (0.89)
  Pallas kernels: 34.7 us -> 30.7 us
    pallas_call x1, Pallas kernels: 34.7 us -> 30.7 us  [body(): pl.pallas_call(functools.partial(kernel, n, slots, 2 * half), out_shape=(...]
where the time goes in v2:
time: 33.6 us; the launch traced here: 33.5 us
  Pallas kernels  30.7 us (91%)
  local copies, waits for them, and re-layouts  2.14 us (6%)
  between operations  0.65 us (2%)
    pallas_call x1, Pallas kernels, body(): pl.pallas_call(functools.partial(kernel, n, slots, 2 * half), out_shape=(...  30.7 us
    unnamed x4, local copies, waits for them, and re-layouts  2.14 us

profile of v2, /device:TPU:0, one launch (start us, length us, event | category | flops | bytes accessed | tf_op | source)
XLA Modules:
  0.0 33.5 jit_solution(10650272237995220550)
XLA Ops:
  0.6 30.7 %shard_map.86 = (bf16[4,128,128]{2,1,0:T(8,128)(2,1)}, bf16[4,128]{1,0:T(4,128)(2,1)}) custom-call(bf16[4,128,128]{2,1,0:T(8,128)(2,1)} %halo.1, s32[4,128]{1,0:T(4,128)} %unmatched.1, s32[4,1,128]{2,1,0:T(1,128)} %bitcast.3, s32[4,16,128]{2,1,0:T(8,128)} %bitcast.2, s32[4,128]{1,0:T(4,128)} %lengths.1, s32[4,128]{1,0:T(4,128)} %choice.1, ...), custom_call_target="tpu_custom_call" | custom-call | tf_op jit(solution)/shard_map/pallas_call | solution.py:323
  31.3 0.0 copy-start
  31.4 1.6 %copy.11 = bf16[4,128,128]{2,1,0:T(8,128)(2,1)} copy(bf16[4,128,128]{2,1,0:T(8,128)(2,1)} %get-tuple-element.4) | data formatting | bytes 262144
  32.9 0.0 copy-done
  32.9 0.6 %copy.12 = bf16[4,128]{1,0:T(4,128)(2,1)} copy(bf16[4,128]{1,0:T(4,128)(2,1)S(1)} %copy-done) | data formatting | bytes 2048
Async XLA Ops:
  31.3 1.6 %copy-start = (bf16[4,128]{1,0:T(4,128)(2,1)S(1)}, bf16[4,128]{1,0:T(4,128)(2,1)}, u32[]{:S(2)}) copy-start(bf16[4,128]{1,0:T(4,128)(2,1)} %get-tuple-element.5) | copy-start | bytes 3076

commit v3 on v2

--- a/solution.py
+++ b/solution.py
@@ -35,11 +35,12 @@
 
 def kernel(
     n, slots, width,
-    halo, unmatched, owner, cand, lengths, choice, desc,
+    halo_in, unmatched_in, owner_in, cand_in, lengths_in, choice_in, desc,
     phantom, best,
+    halo, unmatched, owner, cand, lengths, choice,
     send, recv, send_meta, recv_meta, mine_table, table, scores, bias, taken,
     back, recv_back, back_best, recv_best,
-    row_ss, row_rs, meta_ss, meta_rs, back_ss, back_rs, best_ss, best_rs, table_sem, local_sem,
+    row_ss, row_rs, meta_ss, meta_rs, back_ss, back_rs, best_ss, best_rs, table_sem, local_sem, load_sem,
 ):
     me, core = lax.axis_index("space"), lax.axis_index("rep")
     snaps, halos, half = halo.shape
@@ -58,33 +59,17 @@
             device_id=(peer, core_of(x)), device_id_type=MESH,
         )
 
-    bits = n.bit_length() - 1
-    mine_bits = [lax.rem(lax.div(me, 1 << i), 2) for i in range(bits)]
-
-    def far_first(f):
-        @pl.loop(1, n)
-        def _(d):
-            if n == 1 << bits:
-                m = n - d
-                peer = 0
-                for i in range(bits):
-                    flip = lax.rem(lax.div(m, 1 << i), 2)
-                    peer = peer + (mine_bits[i] + flip - 2 * mine_bits[i] * flip) * (1 << i)
-            else:
-                peer = lax.rem(me + d, n)
-            f(peer)
-
     def each_chip(f):
         @pl.loop(1, n)
         def _(d):
             f(lax.rem(me + d, n))
 
-    def each_peer(f, order=each_chip):
+    def each_peer(f):
         def both(peer):
             f(peer, 0)
             f(peer, 1)
 
-        order(both)
+        each_chip(both)
         f(me, 1)
 
     barrier = pltpu.get_barrier_semaphore()
@@ -92,10 +77,22 @@
         lambda peer, x: pl.semaphore_signal(
             barrier, inc=1, device_id=(peer, core_of(x)), device_id_type=MESH
         ),
-        far_first,
     )
     own_table = pltpu.make_async_copy(desc.at[pl.ds(own * core, own)], mine_table, local_sem.at[0])
     own_table.start()
+    loads = [
+        pltpu.make_async_copy(src, dst, load_sem.at[i])
+        for i, (src, dst) in enumerate(
+            [
+                (owner_in, owner), (unmatched_in, unmatched), (cand_in, cand),
+                (lengths_in, lengths), (choice_in, choice), (halo_in, halo),
+            ]
+        )
+    ]
+    for load in loads:
+        load.start()
+    for load in loads:
+        load.wait()
 
     upper = hot(iota((halos, halos), 0) < iota((halos, halos), 1))
     route = []
@@ -158,9 +155,9 @@
         desc.at[pl.ds(own * core_of(1), own)], table, table_sem.at[0], table_sem.at[1], me, 1
     )
     table_copy.start()
-    far_first(lambda peer: meta_copy(peer, me).start())
-    for ls in range(own):
-        each_peer(lambda peer, x: row_copy(ls, peer, x, me).start(), far_first)
+    each_chip(lambda peer: meta_copy(peer, me).start())
+    for ls in range(own):
+        each_peer(lambda peer, x: row_copy(ls, peer, x, me).start())
     local_meta = pltpu.make_async_copy(send_meta.at[me], recv_meta.at[me], local_sem.at[1])
     local_meta.start()
     local_rows = []
@@ -267,8 +264,8 @@
         fold = term if fold is None else fold + term
         if ls == own - 1:
             back_best[...] = fold.reshape(n, 1, 128)
-            each_peer(lambda peer, x: best_copy(peer, x, me).start(), far_first)
-        each_peer(lambda peer, x: back_copy(ls, peer, x, me).start(), far_first)
+            each_peer(lambda peer, x: best_copy(peer, x, me).start())
+        each_peer(lambda peer, x: back_copy(ls, peer, x, me).start())
         local_backs.append(
             pltpu.make_async_copy(back.at[ls, 0, me], recv_back.at[ls, 0, me], local_sem.at[2 + own + ls])
         )
@@ -313,6 +310,11 @@
     each_peer(lambda peer, x: best_copy(peer, x, me).wait_send())
 
 
+def hand_over(phantom_in, best_in, phantom, best):
+    phantom[...] = phantom_in[...]
+    best[...] = best_in[...]
+
+
 def body(n, halo_rows, unmatched, owner_id, cand_index, lengths, choice_index, desc_rows):
     snaps, halos, half = halo_rows.shape
     cands = desc_rows.shape[1]
@@ -320,15 +322,21 @@
     slots = max(2 * halos // n, 16)
     total = n * slots
     dma = pltpu.SemaphoreType.DMA
-    return pl.pallas_call(
+    results = pl.pallas_call(
         functools.partial(kernel, n, slots, 2 * half),
         out_shape=(
-            jax.ShapeDtypeStruct((snaps, halos, half), BF16),
-            jax.ShapeDtypeStruct((snaps, halos), BF16),
+            pltpu.VMEM((snaps, halos, half), BF16),
+            pltpu.VMEM((snaps, halos), BF16),
         ),
-        in_specs=[pl.BlockSpec(memory_space=pltpu.VMEM)] * 6 + [pl.BlockSpec(memory_space=pl.ANY)],
+        in_specs=[pl.BlockSpec(memory_space=pl.ANY)] * 7,
         out_specs=(pl.BlockSpec(memory_space=pltpu.VMEM),) * 2,
         scratch_shapes=[
+            pltpu.VMEM(halo_rows.shape, BF16),
+            pltpu.VMEM(unmatched.shape, jnp.int32),
+            pltpu.VMEM((snaps, 1, halos), jnp.int32),
+            pltpu.VMEM((snaps, cand_index.shape[2], halos), jnp.int32),
+            pltpu.VMEM(lengths.shape, jnp.int32),
+            pltpu.VMEM(choice_index.shape, jnp.int32),
             pltpu.VMEM((own, 2, n, slots, half), BF16),
             pltpu.VMEM((own, 2, n, slots, half), BF16),
             pltpu.VMEM((n, slots // 2, 128), BF16),
@@ -344,7 +352,7 @@
             pltpu.VMEM((2, n, 1, 128), F32),
             dma((own, 2, n)), dma((own, 2, n)), dma((n,)), dma((n,)),
             dma((own, 2, n)), dma((own, 2, n)), dma((2, n)), dma((2, n)),
-            dma((2,)), dma((3 + 2 * own,)),
+            dma((2,)), dma((3 + 2 * own,)), dma((6,)),
         ],
         compiler_params=pltpu.CompilerParams(collective_id=0, has_side_effects=True),
     )(
@@ -356,6 +364,13 @@
         choice_index,
         desc_rows,
     )
+    shapes = tuple(jax.ShapeDtypeStruct(v.shape, v.dtype) for v in results)
+    return pl.pallas_call(
+        hand_over,
+        out_shape=shapes,
+        in_specs=[pl.BlockSpec(memory_space=pltpu.VMEM)] * 2,
+        out_specs=(pl.BlockSpec(memory_space=pltpu.VMEM),) * 2,
+    )(*[pltpu.with_memory_space_constraint(v, pltpu.VMEM) for v in results])
 
 
 def solution(mesh):

time: 33.6 us -> 30.5 us (0.908)
  local copies, waits for them, and re-layouts: 2.14 us -> 0 us
  Pallas kernels: 30.7 us -> 29.7 us
    unnamed x4 -> x0, local copies, waits for them, and re-layouts: 2.14 us -> none
    pallas_call x1, Pallas kernels: 30.7 us -> 29 us  [body(): pl.pallas_call(functools.partial(kernel, n, slots, 2 * half), out_shape=(...]
    pallas_call x0 -> x1, Pallas kernels: none -> 0.67 us  [body(): pl.pallas_call(hand_over, out_shape=shapes, in_specs=[pl.BlockSpec(memory...]
where the time goes in v3:
time: 30.5 us; the launch traced here: 30.4 us
  Pallas kernels  29.7 us (97%)
  between operations  0.64 us (2%)
    pallas_call x1, Pallas kernels, body(): pl.pallas_call(functools.partial(kernel, n, slots, 2 * half), out_shape=(...  29 us
    pallas_call x1, Pallas kernels, body(): pl.pallas_call(hand_over, out_shape=shapes, in_specs=[pl.BlockSpec(memory...  0.67 us

profile of v3, /device:TPU:0, one launch (start us, length us, event | category | flops | bytes accessed | tf_op | source)
XLA Modules:
  0.0 30.4 jit_solution(16636826928156589065)
XLA Ops:
  0.6 29.0 %shard_map.86 = (bf16[4,128,128]{2,1,0:T(8,128)(2,1)S(1)}, bf16[4,128]{1,0:T(4,128)(2,1)S(1)}) custom-call(bf16[4,128,128]{2,1,0:T(8,128)(2,1)} %halo_in.1, s32[4,128]{1,0:T(4,128)} %unmatched_in.1, s32[4,1,128]{2,1,0:T(1,128)} %bitcast.3, s32[4,16,128]{2,1,0:T(8,128)} %bitcast.2, s32[4,128]{1,0:T(4,128)} %lengths_in.1, s32[4,128]{1,0:T(4,128)} %choice_in.1, ...), custom_call_target="tpu_custom_call" | custom-call | tf_op jit(solution)/shard_map/pallas_call | solution.py:325
  29.7 0.7 %shard_map.87 = (bf16[4,128,128]{2,1,0:T(8,128)(2,1)}, bf16[4,128]{1,0:T(4,128)(2,1)}) custom-call(bf16[4,128,128]{2,1,0:T(8,128)(2,1)S(1)} %get-tuple-element.4.phantom_in, bf16[4,128]{1,0:T(4,128)(2,1)S(1)} %get-tuple-element.5.best_in), custom_call_target="tpu_custom_call" | custom-call | tf_op jit(solution)/shard_map/pallas_call | solution.py:368
